TPU v7x, 32 devices: a whole 2x2x4 slice. The times are simulated.
32 devices in a mesh: narrow: 4 (over z), wide: 8 (over y, x, core).
Axes of the slice: x: 2, y: 2, z: 4, core: 2. Of those that a mesh axis runs over, the one named last changes fastest.
Arguments:
- hidden_in: bfloat16 [8, 2048, 2048], P('narrow', 'wide'), may hold values from -6 to 6
- out_grad: bfloat16 [8, 2048, 2048], P('narrow', 'wide'), may hold values from -6 to 6
- doc_lengths: int32 [8, 8], P('narrow'), may hold values from 1 to 1024, 2048 in all within a row
- attn_gain: bfloat16 [2048], P('narrow'), may hold values from 0.5 to 1.5
- w_query: bfloat16 [2048, 2048], P('narrow', 'wide'), may hold values from -0.125 to 0.125
- w_key: bfloat16 [2048, 2048], P('narrow', 'wide'), may hold values from -0.125 to 0.125
- w_value: bfloat16 [2048, 2048], P('narrow', 'wide'), may hold values from -0.125 to 0.125
- w_out: bfloat16 [2048, 2048], P('wide', 'narrow'), may hold values from -1 to 1
- mlp_gain: bfloat16 [2048], P('narrow'), may hold values from 0.5 to 1.5
- w_gate: bfloat16 [2048, 8192], P('narrow', 'wide'), may hold values from -0.125 to 0.125
- w_up: bfloat16 [2048, 8192], P('narrow', 'wide'), may hold values from -0.125 to 0.125
- w_down: bfloat16 [8192, 2048], P('wide', 'narrow'), may hold values from -0.0625 to 0.0625
Outputs:
- hidden_out: bfloat16 [8, 2048, 2048], P('narrow', 'wide')
- in_grad: bfloat16 [8, 2048, 2048], P('narrow', 'wide')
- grad_attn_gain: float32 [2048], P(('narrow', 'wide'))
- grad_w_query: float32 [2048, 2048], P('narrow', 'wide')
- grad_w_key: float32 [2048, 2048], P('narrow', 'wide')
- grad_w_value: float32 [2048, 2048], P('narrow', 'wide')
- grad_w_out: float32 [2048, 2048], P('wide', 'narrow')
- grad_mlp_gain: float32 [2048], P(('narrow', 'wide'))
- grad_w_gate: float32 [2048, 8192], P('narrow', 'wide')
- grad_w_up: float32 [2048, 8192], P('narrow', 'wide')
- grad_w_down: float32 [8192, 2048], P('wide', 'narrow')
Inputs may be any that keep to these rules, and one draw needn't show every extreme that they name: `doc_lengths`: in every row the 8 lengths sum to 2048, and the longest is exactly 1024.
All inputs are finite; a program needn't handle non-finite values.
Results may differ from a plain program's by a relative error of at most 0.029.
Values may be sent and summed in bfloat16 or wider, within the bound.
No kernel may reach another device: no remote copies, remote signals or barrier semaphores. Data moves between devices by JAX's collectives and lax.ppermute only.
A program may use at most 192 MiB of HBM per device.

v0:
```python
import jax
import jax.numpy as jnp
from jax import lax
from jax.sharding import PartitionSpec as P

HEAD_DIM = 64
EPS = 1e-05
NEG = -1e30
ROPE_BASE = 130000.0


def mat_plain(left_op, right_op):
    return jnp.dot(left_op, right_op, preferred_element_type=jnp.float32)


def mat_back(left_op, right_op):
    return lax.dot_general(
        left_op, right_op, (((1,), (1,)), ((), ())), preferred_element_type=jnp.float32
    )


def mat_outer(left_op, right_op):
    return lax.dot_general(
        left_op, right_op, (((0,), (0,)), ((), ())), preferred_element_type=jnp.float32
    )


def rounded(values_in):
    return values_in.astype(jnp.bfloat16).astype(jnp.float32)


def doc_starts(lengths, seq_len):
    tokens = jnp.arange(seq_len, dtype=jnp.int32)
    ends_at = jnp.cumsum(lengths)
    before = jnp.where(ends_at[None, :] <= tokens[:, None], ends_at[None, :], jnp.int32(0))
    return jnp.max(before, axis=1)


def rope_tables(starts, seq_len):
    half_dim = HEAD_DIM // 2
    position = (jnp.arange(seq_len, dtype=jnp.int32) - starts).astype(jnp.float32)
    inverse = ROPE_BASE ** (-(jnp.arange(half_dim, dtype=jnp.float32) * 2.0) / HEAD_DIM)
    angles = position[:, None] * inverse[None, :]
    return (jnp.cos(angles)[:, None, :], jnp.sin(angles)[:, None, :])


def rotate(tensor, cos_table, sin_table):
    half_dim = tensor.shape[-1] // 2
    front_half = tensor[..., :half_dim]
    back_half = tensor[..., half_dim:]
    return jnp.concatenate(
        [
            front_half * cos_table - back_half * sin_table,
            back_half * cos_table + front_half * sin_table,
        ],
        axis=-1,
    )


def allowed_keys(starts, first_row, block_len, seq_len):
    row_ids = first_row + jnp.arange(block_len, dtype=jnp.int32)
    columns = jnp.arange(seq_len, dtype=jnp.int32)
    begins = lax.dynamic_slice_in_dim(starts, first_row, block_len)
    return (columns[None, :] <= row_ids[:, None]) & (columns[None, :] >= begins[:, None])


def attend_forward(queries, keys_rot, values_in, starts, block_len):
    seq_len, heads_here, head_size = queries.shape
    n_blocks = seq_len // block_len
    score_scale = head_size ** (-0.5)
    blocks = queries.reshape(n_blocks, block_len, heads_here, head_size)
    firsts = jnp.arange(n_blocks, dtype=jnp.int32) * block_len

    def one_block(block_pair):
        q_block, first_row = block_pair
        allowed = allowed_keys(starts, first_row, block_len, seq_len)
        scores = (
            jnp.einsum("qhd,khd->hqk", q_block, keys_rot, preferred_element_type=jnp.float32)
            * score_scale
        )
        masked = jnp.where(allowed[None], scores, NEG)
        row_max = jnp.max(masked, axis=-1, keepdims=True)
        exp_terms = jnp.exp(masked - row_max)
        row_total = jnp.sum(exp_terms, axis=-1, keepdims=True)
        prob_rows = (exp_terms / row_total).astype(jnp.bfloat16)
        block_out = jnp.einsum(
            "hqk,khd->qhd", prob_rows, values_in, preferred_element_type=jnp.float32
        )
        return (block_out, (row_max + jnp.log(row_total))[..., 0])

    block_outs, log_totals = lax.map(one_block, (blocks, firsts))
    return (block_outs.reshape(seq_len, heads_here * head_size), log_totals)


def attend_backward(queries, keys_rot, values_in, grad_att, log_totals, starts, block_len):
    seq_len, heads_here, head_size = queries.shape
    n_blocks = seq_len // block_len
    score_scale = head_size ** (-0.5)
    q_blocks = queries.reshape(n_blocks, block_len, heads_here, head_size)
    g_blocks = grad_att.reshape(n_blocks, block_len, heads_here, head_size)
    firsts = jnp.arange(n_blocks, dtype=jnp.int32) * block_len

    def one_block(carried, block_pack):
        key_acc, value_acc = carried
        q_block, g_block, lse_block, first_row = block_pack
        allowed = allowed_keys(starts, first_row, block_len, seq_len)
        scores = (
            jnp.einsum("qhd,khd->hqk", q_block, keys_rot, preferred_element_type=jnp.float32)
            * score_scale
        )
        masked = jnp.where(allowed[None], scores, NEG)
        probs_full = jnp.exp(masked - lse_block[..., None])
        prob_rows = probs_full.astype(jnp.bfloat16)
        value_acc = value_acc + jnp.einsum(
            "hqk,qhd->khd", prob_rows, g_block, preferred_element_type=jnp.float32
        )
        grad_probs = jnp.einsum(
            "qhd,khd->hqk", g_block, values_in, preferred_element_type=jnp.float32
        )
        row_inner = jnp.sum(probs_full * grad_probs, axis=-1, keepdims=True)
        grad_scores = (probs_full * (grad_probs - row_inner)).astype(jnp.bfloat16)
        query_grad = (
            jnp.einsum("hqk,khd->qhd", grad_scores, keys_rot, preferred_element_type=jnp.float32)
            * score_scale
        )
        key_acc = (
            key_acc
            + jnp.einsum("hqk,qhd->khd", grad_scores, q_block, preferred_element_type=jnp.float32)
            * score_scale
        )
        return ((key_acc, value_acc), query_grad)

    zero_field = jnp.zeros((seq_len, heads_here, head_size), jnp.float32)
    (key_grad, value_grad), query_grads = lax.scan(
        one_block, (zero_field, zero_field), (q_blocks, g_blocks, log_totals, firsts)
    )
    return (query_grads.reshape(seq_len, heads_here, head_size), key_grad, value_grad)


def one_row(input_row, grad_row, lengths, weights):
    inner_set, outer_set = weights
    w_query, w_key, w_value, w_gate, w_up, gain_attn, gain_mlp = inner_set
    w_out, w_down = outer_set
    attn_scale = gain_attn.astype(jnp.float32)
    mlp_scale = gain_mlp.astype(jnp.float32)
    local_rows = input_row.shape[0]
    seq_len = local_rows * lax.axis_size("wide")
    heads_here = w_query.shape[1] // HEAD_DIM
    block_len = min(512, seq_len)
    field_shape = (seq_len, heads_here, HEAD_DIM)
    flat_shape = (seq_len, heads_here * HEAD_DIM)
    starts = doc_starts(lengths, seq_len)
    cos_table, sin_table = rope_tables(starts, seq_len)
    residual = input_row.astype(jnp.float32)
    inv_first = lax.rsqrt(jnp.mean(residual * residual, axis=-1, keepdims=True) + EPS)
    normed = residual * inv_first
    attn_in = lax.all_gather((normed * attn_scale).astype(jnp.bfloat16), "wide", axis=0, tiled=True)
    queries = rotate(mat_plain(attn_in, w_query).reshape(field_shape), cos_table, sin_table).astype(
        jnp.bfloat16
    )
    keys_rot = rotate(mat_plain(attn_in, w_key).reshape(field_shape), cos_table, sin_table).astype(
        jnp.bfloat16
    )
    values_in = mat_plain(attn_in, w_value).astype(jnp.bfloat16).reshape(field_shape)
    attended, log_totals = attend_forward(queries, keys_rot, values_in, starts, block_len)
    attended = attended.astype(jnp.bfloat16)
    middle = residual + lax.psum_scatter(
        rounded(mat_plain(attended, w_out)).astype(jnp.bfloat16),
        "wide",
        scatter_dimension=0,
        tiled=True,
    ).astype(jnp.float32)
    inv_second = lax.rsqrt(jnp.mean(middle * middle, axis=-1, keepdims=True) + EPS)
    normed_mid = middle * inv_second
    mlp_in = lax.all_gather(
        (normed_mid * mlp_scale).astype(jnp.bfloat16), "wide", axis=0, tiled=True
    )
    gate_pre = mat_plain(mlp_in, w_gate)
    up_pre = mat_plain(mlp_in, w_up)
    sigmoid_gate = jax.nn.sigmoid(gate_pre)
    silu_gate = gate_pre * sigmoid_gate
    hidden = (silu_gate * up_pre).astype(jnp.bfloat16)
    output = middle + lax.psum_scatter(
        rounded(mat_plain(hidden, w_down)).astype(jnp.bfloat16),
        "wide",
        scatter_dimension=0,
        tiled=True,
    ).astype(jnp.float32)
    grad_full = lax.all_gather(grad_row, "wide", axis=0, tiled=True)
    grad_down = mat_outer(hidden, grad_full)
    grad_hidden = mat_back(grad_full, w_down)
    grad_gate_pre = (
        grad_hidden * up_pre * sigmoid_gate * (1.0 + gate_pre * (1.0 - sigmoid_gate))
    ).astype(jnp.bfloat16)
    grad_up_pre = (grad_hidden * silu_gate).astype(jnp.bfloat16)
    grad_gate = mat_outer(mlp_in, grad_gate_pre)
    grad_up = mat_outer(mlp_in, grad_up_pre)
    grad_mlp_in = lax.psum_scatter(
        rounded(mat_back(grad_gate_pre, w_gate) + mat_back(grad_up_pre, w_up)).astype(jnp.bfloat16),
        "wide",
        scatter_dimension=0,
        tiled=True,
    ).astype(jnp.float32)
    scaled_mid = grad_mlp_in * mlp_scale
    gain_mlp_grad = jnp.sum(grad_mlp_in * normed_mid, axis=0)
    grad_middle = grad_row.astype(jnp.float32) + inv_second * (
        scaled_mid - normed_mid * jnp.mean(scaled_mid * normed_mid, axis=-1, keepdims=True)
    )
    grad_branch = lax.all_gather(grad_middle.astype(jnp.bfloat16), "wide", axis=0, tiled=True)
    grad_out = mat_outer(attended, grad_branch)
    grad_att = mat_back(grad_branch, w_out).astype(jnp.bfloat16).reshape(field_shape)
    query_grad, key_grad, value_grad = attend_backward(
        queries, keys_rot, values_in, grad_att, log_totals, starts, block_len
    )
    query_raw = rotate(query_grad, cos_table, -sin_table).reshape(flat_shape).astype(jnp.bfloat16)
    key_raw = rotate(key_grad, cos_table, -sin_table).reshape(flat_shape).astype(jnp.bfloat16)
    value_raw = value_grad.reshape(flat_shape).astype(jnp.bfloat16)
    grad_query = mat_outer(attn_in, query_raw)
    grad_key = mat_outer(attn_in, key_raw)
    grad_value = mat_outer(attn_in, value_raw)
    grad_attn_in = lax.psum_scatter(
        rounded(
            mat_back(query_raw, w_query) + mat_back(key_raw, w_key) + mat_back(value_raw, w_value)
        ).astype(jnp.bfloat16),
        "wide",
        scatter_dimension=0,
        tiled=True,
    ).astype(jnp.float32)
    scaled_in = grad_attn_in * attn_scale
    gain_attn_grad = jnp.sum(grad_attn_in * normed, axis=0)
    grad_input = grad_middle + inv_first * (
        scaled_in - normed * jnp.mean(scaled_in * normed, axis=-1, keepdims=True)
    )
    return (
        output.astype(jnp.bfloat16),
        grad_input.astype(jnp.bfloat16),
        (grad_query, grad_key, grad_value, grad_gate, grad_up),
        (grad_out, grad_down),
        (gain_attn_grad, gain_mlp_grad),
    )


def per_device(
    hidden_in,
    out_grad,
    doc_lengths,
    attn_gain,
    w_query,
    w_key,
    w_value,
    w_out,
    mlp_gain,
    w_gate,
    w_up,
    w_down,
):
    narrow_count = lax.axis_size("narrow")

    def fetch_weights():
        inner_set = (
            lax.all_gather(w_query, "narrow", axis=0, tiled=True),
            lax.all_gather(w_key, "narrow", axis=0, tiled=True),
            lax.all_gather(w_value, "narrow", axis=0, tiled=True),
            lax.all_gather(w_gate, "narrow", axis=0, tiled=True),
            lax.all_gather(w_up, "narrow", axis=0, tiled=True),
            lax.all_gather(attn_gain, "narrow", axis=0, tiled=True),
            lax.all_gather(mlp_gain, "narrow", axis=0, tiled=True),
        )
        outer_set = (
            lax.all_gather(w_out, "narrow", axis=1, tiled=True),
            lax.all_gather(w_down, "narrow", axis=1, tiled=True),
        )
        return (inner_set, outer_set)

    def share_grads(grads_in, grads_out):
        summed_in = (
            lax.psum_scatter(
                grads_in[0].astype(jnp.bfloat16), "narrow", scatter_dimension=0, tiled=True
            ).astype(jnp.float32),
            lax.psum_scatter(
                grads_in[1].astype(jnp.bfloat16), "narrow", scatter_dimension=0, tiled=True
            ).astype(jnp.float32),
            lax.psum_scatter(
                grads_in[2].astype(jnp.bfloat16), "narrow", scatter_dimension=0, tiled=True
            ).astype(jnp.float32),
            lax.psum_scatter(
                grads_in[3].astype(jnp.bfloat16), "narrow", scatter_dimension=0, tiled=True
            ).astype(jnp.float32),
            lax.psum_scatter(
                grads_in[4].astype(jnp.bfloat16), "narrow", scatter_dimension=0, tiled=True
            ).astype(jnp.float32),
        )
        summed_out = (
            lax.psum_scatter(
                grads_out[0].astype(jnp.bfloat16), "narrow", scatter_dimension=1, tiled=True
            ).astype(jnp.float32),
            lax.psum_scatter(
                grads_out[1].astype(jnp.bfloat16), "narrow", scatter_dimension=1, tiled=True
            ).astype(jnp.float32),
        )
        return (summed_in, summed_out)

    acc_in = tuple(
        (jnp.zeros(weight.shape, jnp.float32) for weight in (w_query, w_key, w_value, w_gate, w_up))
    )
    acc_out = tuple((jnp.zeros(weight.shape, jnp.float32) for weight in (w_out, w_down)))
    gain_acc = (
        jnp.zeros((attn_gain.shape[0] * narrow_count,), jnp.float32),
        jnp.zeros((mlp_gain.shape[0] * narrow_count,), jnp.float32),
    )

    def micro_step(carried, inputs):
        sum_in, sum_out, sum_gain = carried
        input_row, grad_row, lengths = inputs
        weights = fetch_weights()
        output, grad_input, grads_in, grads_out, grads_gain = one_row(
            input_row, grad_row, lengths, weights
        )
        grads_in, grads_out = share_grads(grads_in, grads_out)
        sum_in = tuple((acc_item + new_item for acc_item, new_item in zip(sum_in, grads_in)))
        sum_out = tuple((acc_item + new_item for acc_item, new_item in zip(sum_out, grads_out)))
        sum_gain = tuple((acc_item + new_item for acc_item, new_item in zip(sum_gain, grads_gain)))
        return ((sum_in, sum_out, sum_gain), (output, grad_input))

    carried, (outputs, in_grads) = lax.scan(
        micro_step, (acc_in, acc_out, gain_acc), (hidden_in, out_grad, doc_lengths)
    )
    sum_in, sum_out, sum_gain = carried
    gain_grads = (
        lax.psum_scatter(sum_gain[0], ("narrow", "wide"), scatter_dimension=0, tiled=True),
        lax.psum_scatter(sum_gain[1], ("narrow", "wide"), scatter_dimension=0, tiled=True),
    )
    return (
        outputs,
        in_grads,
        gain_grads[0],
        sum_in[0],
        sum_in[1],
        sum_in[2],
        sum_out[0],
        gain_grads[1],
        sum_in[3],
        sum_in[4],
        sum_out[1],
    )


def solution(mesh):
    in_specs = (
        P("narrow", "wide", None),
        P("narrow", "wide", None),
        P("narrow", None),
        P("narrow"),
        P("narrow", "wide"),
        P("narrow", "wide"),
        P("narrow", "wide"),
        P("wide", "narrow"),
        P("narrow"),
        P("narrow", "wide"),
        P("narrow", "wide"),
        P("wide", "narrow"),
    )
    out_specs = (
        P("narrow", "wide", None),
        P("narrow", "wide", None),
        P(("narrow", "wide")),
        P("narrow", "wide"),
        P("narrow", "wide"),
        P("narrow", "wide"),
        P("wide", "narrow"),
        P(("narrow", "wide")),
        P("narrow", "wide"),
        P("narrow", "wide"),
        P("wide", "narrow"),
    )
    return jax.shard_map(
        per_device, mesh=mesh, in_specs=in_specs, out_specs=out_specs, check_vma=False
    )
```

profile of v0, /device:TPU:0, one launch (start us, length us, event | category | flops | bytes accessed | tf_op | source)
XLA Modules:
  0.0 2786.1 jit_solution(1502561951740328314)
XLA Ops:
  7.3 2731.1 %while.62 = (s32[]{:T(128)}, f32[512,256]{1,0:T(8,128)}, f32[512,256]{1,0:T(8,128)}, f32[512,256]{1,0:T(8,128)}, f32[512,1024]{1,0:T(8,128)}, /*index=5*/f32[512...) while((s32[]{:T(128)}, f32[512,256]{1,0:T(8,128)}, ...), condition=%wide.region_27.28_spmd.clone, body=%wide.region_0.27_spmd.clone.sunk | while | flops 107088232448 | bytes 1211792128 | solution.py:325
  40.8 55.8 %all-gather.24.cloned.1.call-done = bf16[2048,2048]{1,0:T(8,128)(2,1)} async-done(((bf16[256,2048]{1,0:T(8,128)(2,1)}), bf16[2048,2048]{1,0:T(8,128)(2,1)}) %all-gather.24.cloned.1.call-update) | async-done | bytes 8388624 | tf_op jit(solution)/shard_map/while/body/eval_jaxpr/all_gather | solution.py:157
  102.6 23.6 all-gather.26.cloned.1.call-done
  133.0 22.1 all-gather.30.cloned.1.call-done
  161.1 74.7 %while.63 = (s32[]{:T(128)}, bf16[4,512,4,64]{1,3,2,0:T(8,128)(2,1)}, f32[4,4,512]{2,1,0:T(4,128)}, s32[4]{0:T(128)S(1)}, s32[2048]{0:T(1024)}, /*index=5*/bf16[...) while((s32[]{:T(128)}, ...), condition=%wide.region_7.7_spmd, body=%wide.region_4.6_spmd.sunk | while | flops 1127217664 | bytes 65874156 | solution.py:91
  263.1 54.9 %reduce-scatter.12.cloned.1.call-done = bf16[256,2048]{1,0:T(8,128)(2,1)} async-done(((bf16[2048,2048]{1,0:T(8,128)(2,1)}), bf16[256,2048]{1,0:T(8,128)(2,1)}) %reduce-scatter.12.cloned.1.call-update) | async-done | bytes 1048592 | tf_op jit(solution)/shard_map/while/body/eval_jaxpr/reduce_scatter | solution.py:167
  323.1 77.4 %all-gather.38.cloned.1.call-done = bf16[1024,2048]{1,0:T(8,128)(2,1)} async-done(((bf16[1024,512]{1,0:T(8,128)(2,1)}), bf16[1024,2048]{1,0:T(8,128)(2,1)}) %all-gather.38.cloned.1.call-update) | async-done | bytes 4194320 | tf_op jit(solution)/shard_map/while/body/eval_jaxpr/all_gather | solution.py:271
  400.4 55.0 %all-gather.40.cloned.1.call-done = bf16[1,2048,2048]{2,1,0:T(8,128)(2,1)} async-done(((bf16[1,256,2048]{2,1,0:T(8,128)(2,1)}), bf16[1,2048,2048]{2,1,0:T(8,128)(2,1)}) %all-gather.40.cloned.1.call-update) | async-done | bytes 8388624 | tf_op jit(solution)/shard_map/while/body/eval_jaxpr/all_gather | solution.py:189
  470.1 67.7 %all-gather.36.cloned.1.call-done = bf16[2048,1024]{1,0:T(8,128)(2,1)} async-done(((bf16[512,1024]{1,0:T(8,128)(2,1)}), bf16[2048,1024]{1,0:T(8,128)(2,1)}) %all-gather.36.cloned.1.call-update) | async-done | bytes 4194320 | tf_op jit(solution)/shard_map/while/body/eval_jaxpr/all_gather | solution.py:264
  537.9 54.8 %all-gather.34.cloned.1.call-done = bf16[2048,2048]{1,0:T(8,128)(2,1)} async-done(((bf16[256,2048]{1,0:T(8,128)(2,1)}), bf16[2048,2048]{1,0:T(8,128)(2,1)}) %all-gather.34.cloned.1.call-update) | async-done | bytes 8388624 | tf_op jit(solution)/shard_map/while/body/eval_jaxpr/all_gather | solution.py:175
  607.1 68.1 %all-gather.42.cloned.1.call-done = bf16[2048,1024]{1,0:T(8,128)(2,1)} async-done(((bf16[512,1024]{1,0:T(8,128)(2,1)}), bf16[2048,1024]{1,0:T(8,128)(2,1)}) %all-gather.42.cloned.1.call-update) | async-done | bytes 4194320 | tf_op jit(solution)/shard_map/while/body/eval_jaxpr/all_gather | solution.py:265
  675.2 21.8 multiply_convert_fusion.9
  727.9 69.9 %reduce-scatter.14.cloned.1.call-done = bf16[256,2048]{1,0:T(8,128)(2,1)} async-done(((bf16[2048,2048]{1,0:T(8,128)(2,1)}), bf16[256,2048]{1,0:T(8,128)(2,1)}) %reduce-scatter.14.cloned.1.call-update) | async-done | bytes 1048592 | tf_op jit(solution)/shard_map/while/body/eval_jaxpr/reduce_scatter | solution.py:198
  875.4 249.1 %while.64 = (s32[]{:T(128)}, f32[2048,4,64]{0,2,1:T(8,128)}, f32[2048,4,64]{0,2,1:T(8,128)}, f32[4,512,4,64]{1,0,3,2:T(4,128)}, bf16[4,512,4,64]{1,3,2,0:T(8,128...) while((s32[]{:T(128)}, f32[2048,4,64]{0,2,1:T(8,128)}, ...), condition=%wide.region_14.14_spmd.clone, body=%wide.region_12.13_spmd.clone.sunk | while | flops 2753165824 | bytes 183044368 | solution.py:134
  1221.5 72.0 %reduce-scatter.30.cloned.1.call-done = bf16[256,2048]{1,0:T(8,128)(2,1)} async-done(((bf16[2048,2048]{1,0:T(8,128)(2,1)}), bf16[256,2048]{1,0:T(8,128)(2,1)}) %reduce-scatter.30.cloned.1.call-update) | async-done | bytes 1048592 | tf_op jit(solution)/shard_map/while/body/eval_jaxpr/reduce_scatter | solution.py:221
  1295.6 72.7 %reduce-scatter.32.cloned.1.call-done = bf16[256,2048]{1,0:T(8,128)(2,1)} async-done(((bf16[2048,2048]{1,0:T(8,128)(2,1)}), bf16[256,2048]{1,0:T(8,128)(2,1)}) %reduce-scatter.32.cloned.1.call-update) | async-done | bytes 1048592 | tf_op jit(solution)/shard_map/while/body/eval_jaxpr/reduce_scatter | solution.py:183
  1404.3 55.7 %all-gather.24.cloned.1.call-done = bf16[2048,2048]{1,0:T(8,128)(2,1)} async-done(((bf16[256,2048]{1,0:T(8,128)(2,1)}), bf16[2048,2048]{1,0:T(8,128)(2,1)}) %all-gather.24.cloned.1.call-update) | async-done | bytes 8388624 | tf_op jit(solution)/shard_map/while/body/eval_jaxpr/all_gather | solution.py:157
  1466.0 23.5 all-gather.26.cloned.1.call-done
  1496.3 22.1 all-gather.30.cloned.1.call-done
  1524.4 74.7 %while.63 = (s32[]{:T(128)}, bf16[4,512,4,64]{1,3,2,0:T(8,128)(2,1)}, f32[4,4,512]{2,1,0:T(4,128)}, s32[4]{0:T(128)S(1)}, s32[2048]{0:T(1024)}, /*index=5*/bf16[...) while((s32[]{:T(128)}, ...), condition=%wide.region_7.7_spmd, body=%wide.region_4.6_spmd.sunk | while | flops 1127217664 | bytes 65874156 | solution.py:91
  1626.5 54.8 %reduce-scatter.12.cloned.1.call-done = bf16[256,2048]{1,0:T(8,128)(2,1)} async-done(((bf16[2048,2048]{1,0:T(8,128)(2,1)}), bf16[256,2048]{1,0:T(8,128)(2,1)}) %reduce-scatter.12.cloned.1.call-update) | async-done | bytes 1048592 | tf_op jit(solution)/shard_map/while/body/eval_jaxpr/reduce_scatter | solution.py:167
  1686.2 77.5 %all-gather.38.cloned.1.call-done = bf16[1024,2048]{1,0:T(8,128)(2,1)} async-done(((bf16[1024,512]{1,0:T(8,128)(2,1)}), bf16[1024,2048]{1,0:T(8,128)(2,1)}) %all-gather.38.cloned.1.call-update) | async-done | bytes 4194320 | tf_op jit(solution)/shard_map/while/body/eval_jaxpr/all_gather | solution.py:271
  1763.7 54.8 %all-gather.40.cloned.1.call-done = bf16[1,2048,2048]{2,1,0:T(8,128)(2,1)} async-done(((bf16[1,256,2048]{2,1,0:T(8,128)(2,1)}), bf16[1,2048,2048]{2,1,0:T(8,128)(2,1)}) %all-gather.40.cloned.1.call-update) | async-done | bytes 8388624 | tf_op jit(solution)/shard_map/while/body/eval_jaxpr/all_gather | solution.py:189
  1833.3 67.7 %all-gather.36.cloned.1.call-done = bf16[2048,1024]{1,0:T(8,128)(2,1)} async-done(((bf16[512,1024]{1,0:T(8,128)(2,1)}), bf16[2048,1024]{1,0:T(8,128)(2,1)}) %all-gather.36.cloned.1.call-update) | async-done | bytes 4194320 | tf_op jit(solution)/shard_map/while/body/eval_jaxpr/all_gather | solution.py:264
  1901.0 55.0 %all-gather.34.cloned.1.call-done = bf16[2048,2048]{1,0:T(8,128)(2,1)} async-done(((bf16[256,2048]{1,0:T(8,128)(2,1)}), bf16[2048,2048]{1,0:T(8,128)(2,1)}) %all-gather.34.cloned.1.call-update) | async-done | bytes 8388624 | tf_op jit(solution)/shard_map/while/body/eval_jaxpr/all_gather | solution.py:175
  1970.4 67.9 %all-gather.42.cloned.1.call-done = bf16[2048,1024]{1,0:T(8,128)(2,1)} async-done(((bf16[512,1024]{1,0:T(8,128)(2,1)}), bf16[2048,1024]{1,0:T(8,128)(2,1)}) %all-gather.42.cloned.1.call-update) | async-done | bytes 4194320 | tf_op jit(solution)/shard_map/while/body/eval_jaxpr/all_gather | solution.py:265
  2038.3 21.8 multiply_convert_fusion.9
  2091.0 69.9 %reduce-scatter.14.cloned.1.call-done = bf16[256,2048]{1,0:T(8,128)(2,1)} async-done(((bf16[2048,2048]{1,0:T(8,128)(2,1)}), bf16[256,2048]{1,0:T(8,128)(2,1)}) %reduce-scatter.14.cloned.1.call-update) | async-done | bytes 1048592 | tf_op jit(solution)/shard_map/while/body/eval_jaxpr/reduce_scatter | solution.py:198
  2238.6 249.0 %while.64 = (s32[]{:T(128)}, f32[2048,4,64]{0,2,1:T(8,128)}, f32[2048,4,64]{0,2,1:T(8,128)}, f32[4,512,4,64]{1,0,3,2:T(4,128)}, bf16[4,512,4,64]{1,3,2,0:T(8,128...) while((s32[]{:T(128)}, f32[2048,4,64]{0,2,1:T(8,128)}, ...), condition=%wide.region_14.14_spmd.clone, body=%wide.region_12.13_spmd.clone.sunk | while | flops 2753165824 | bytes 183044368 | solution.py:134
  2585.0 71.8 %reduce-scatter.30.cloned.1.call-done = bf16[256,2048]{1,0:T(8,128)(2,1)} async-done(((bf16[2048,2048]{1,0:T(8,128)(2,1)}), bf16[256,2048]{1,0:T(8,128)(2,1)}) %reduce-scatter.30.cloned.1.call-update) | async-done | bytes 1048592 | tf_op jit(solution)/shard_map/while/body/eval_jaxpr/reduce_scatter | solution.py:221
  2658.8 72.7 %reduce-scatter.32.cloned.1.call-done = bf16[256,2048]{1,0:T(8,128)(2,1)} async-done(((bf16[2048,2048]{1,0:T(8,128)(2,1)}), bf16[256,2048]{1,0:T(8,128)(2,1)}) %reduce-scatter.32.cloned.1.call-update) | async-done | bytes 1048592 | tf_op jit(solution)/shard_map/while/body/eval_jaxpr/reduce_scatter | solution.py:183
  2738.4 39.7 %all-reduce.2 = (f32[2048]{0:T(1024)S(1)}, f32[2048]{0:T(1024)S(1)}) all-reduce(f32[2048]{0:T(1024)} %get-tuple-element.247, f32[2048]{0:T(1024)} %get-tuple-element.252), channel_id=14, replica_groups=mesh['narrow'=4,'wide'=8] {'narrow','wide'}, use_global_device_ids=true, to_apply=%region_28.29.clone | all-reduce | flops 4096 | bytes 32768
  (649 shorter events, 1263.4 us)
Async XLA Ops:
  28.8 211.0 %all-gather.32.cloned.1.call-start = ((), (), s32[]{:S(2)}) async-start(), calls=%async_computation.15 | async-start | bytes 1310720 | tf_op jit(solution)/shard_map/while/body/eval_jaxpr/all_gather | solution.py:270
  29.3 288.7 %reduce-scatter.12.cloned.1.call-start = ((), (), s32[]{:S(2)}) async-start(), calls=%async_computation.16 | async-start | bytes 9437184 | tf_op jit(solution)/shard_map/while/body/eval_jaxpr/reduce_scatter | solution.py:167
  247.1 153.4 %all-gather.38.cloned.1.call-start = ((), (), s32[]{:S(2)}) async-start(), calls=%async_computation.19 | async-start | bytes 5242880 | tf_op jit(solution)/shard_map/while/body/eval_jaxpr/all_gather | solution.py:271
  247.8 207.6 %all-gather.40.cloned.1.call-start = ((), (), s32[]{:S(2)}) async-start(), calls=%async_computation.20 | async-start | bytes 9437184 | tf_op jit(solution)/shard_map/while/body/eval_jaxpr/all_gather | solution.py:189
  250.2 287.6 %all-gather.36.cloned.1.call-start = ((), (), s32[]{:S(2)}) async-start(), calls=%async_computation.18 | async-start | bytes 5242880 | tf_op jit(solution)/shard_map/while/body/eval_jaxpr/all_gather | solution.py:264
  251.0 341.7 %all-gather.34.cloned.1.call-start = ((), (), s32[]{:S(2)}) async-start(), calls=%async_computation.17 | async-start | bytes 9437184 | tf_op jit(solution)/shard_map/while/body/eval_jaxpr/all_gather | solution.py:175
  322.3 352.9 %all-gather.42.cloned.1.call-start = ((), (), s32[]{:S(2)}) async-start(), calls=%async_computation.21 | async-start | bytes 5242880 | tf_op jit(solution)/shard_map/while/body/eval_jaxpr/all_gather | solution.py:265
  323.0 474.8 %reduce-scatter.14.cloned.1.call-start = ((), (), s32[]{:S(2)}) async-start(), calls=%async_computation.22 | async-start | bytes 9437184 | tf_op jit(solution)/shard_map/while/body/eval_jaxpr/reduce_scatter | solution.py:198
  727.8 131.4 %all-gather.44.cloned.1.call-start = ((), (), s32[]{:S(2)}) async-start(), calls=%async_computation.23 | async-start | bytes 9437184 | tf_op jit(solution)/shard_map/while/body/eval_jaxpr/all_gather | solution.py:209
  804.7 395.0 %reduce-scatter.28.cloned.1.call-start = ((), (), s32[]{:S(2)}) async-start(), calls=%async_computation.30 | async-start | bytes 5242880 | tf_op jit(solution)/shard_map/while/body/eval_jaxpr/reduce_scatter | solution.py:297
  819.0 384.1 %reduce-scatter.22.cloned.1.call-start = ((), (), s32[]{:S(2)}) async-start(), calls=%async_computation.27 | async-start | bytes 5242880 | tf_op jit(solution)/shard_map/while/body/eval_jaxpr/reduce_scatter | solution.py:286
  833.1 373.9 %reduce-scatter.24.cloned.1.call-start = ((), (), s32[]{:S(2)}) async-start(), calls=%async_computation.28 | async-start | bytes 5242880 | tf_op jit(solution)/shard_map/while/body/eval_jaxpr/reduce_scatter | solution.py:289
  847.9 362.4 %reduce-scatter.26.cloned.1.call-start = ((), (), s32[]{:S(2)}) async-start(), calls=%async_computation.29 | async-start | bytes 1310720 | tf_op jit(solution)/shard_map/while/body/eval_jaxpr/reduce_scatter | solution.py:294
  875.4 336.8 %reduce-scatter.18.cloned.1.call-start = ((), (), s32[]{:S(2)}) async-start(), calls=%async_computation.25 | async-start | bytes 1310720 | tf_op jit(solution)/shard_map/while/body/eval_jaxpr/reduce_scatter | solution.py:280
  1151.8 141.7 %reduce-scatter.30.cloned.1.call-start = ((), (), s32[]{:S(2)}) async-start(), calls=%async_computation.31 | async-start | bytes 9437184 | tf_op jit(solution)/shard_map/while/body/eval_jaxpr/reduce_scatter | solution.py:221
  1185.3 183.0 %reduce-scatter.32.cloned.1.call-start = ((), (), s32[]{:S(2)}) async-start(), calls=%async_computation.32 | async-start | bytes 9437184 | tf_op jit(solution)/shard_map/while/body/eval_jaxpr/reduce_scatter | solution.py:183
  1393.3 209.8 %all-gather.32.cloned.1.call-start = ((), (), s32[]{:S(2)}) async-start(), calls=%async_computation.15 | async-start | bytes 1310720 | tf_op jit(solution)/shard_map/while/body/eval_jaxpr/all_gather | solution.py:270
  1393.9 287.4 %reduce-scatter.12.cloned.1.call-start = ((), (), s32[]{:S(2)}) async-start(), calls=%async_computation.16 | async-start | bytes 9437184 | tf_op jit(solution)/shard_map/while/body/eval_jaxpr/reduce_scatter | solution.py:167
  1610.4 153.3 %all-gather.38.cloned.1.call-start = ((), (), s32[]{:S(2)}) async-start(), calls=%async_computation.19 | async-start | bytes 5242880 | tf_op jit(solution)/shard_map/while/body/eval_jaxpr/all_gather | solution.py:271
  1611.1 207.4 %all-gather.40.cloned.1.call-start = ((), (), s32[]{:S(2)}) async-start(), calls=%async_computation.20 | async-start | bytes 9437184 | tf_op jit(solution)/shard_map/while/body/eval_jaxpr/all_gather | solution.py:189
  1613.5 287.5 %all-gather.36.cloned.1.call-start = ((), (), s32[]{:S(2)}) async-start(), calls=%async_computation.18 | async-start | bytes 5242880 | tf_op jit(solution)/shard_map/while/body/eval_jaxpr/all_gather | solution.py:264
  1614.3 341.7 %all-gather.34.cloned.1.call-start = ((), (), s32[]{:S(2)}) async-start(), calls=%async_computation.17 | async-start | bytes 9437184 | tf_op jit(solution)/shard_map/while/body/eval_jaxpr/all_gather | solution.py:175
  1685.6 352.8 %all-gather.42.cloned.1.call-start = ((), (), s32[]{:S(2)}) async-start(), calls=%async_computation.21 | async-start | bytes 5242880 | tf_op jit(solution)/shard_map/while/body/eval_jaxpr/all_gather | solution.py:265
  1686.2 474.8 %reduce-scatter.14.cloned.1.call-start = ((), (), s32[]{:S(2)}) async-start(), calls=%async_computation.22 | async-start | bytes 9437184 | tf_op jit(solution)/shard_map/while/body/eval_jaxpr/reduce_scatter | solution.py:198
  2091.0 131.4 %all-gather.44.cloned.1.call-start = ((), (), s32[]{:S(2)}) async-start(), calls=%async_computation.23 | async-start | bytes 9437184 | tf_op jit(solution)/shard_map/while/body/eval_jaxpr/all_gather | solution.py:209
  2167.9 395.0 %reduce-scatter.28.cloned.1.call-start = ((), (), s32[]{:S(2)}) async-start(), calls=%async_computation.30 | async-start | bytes 5242880 | tf_op jit(solution)/shard_map/while/body/eval_jaxpr/reduce_scatter | solution.py:297
  2182.2 384.1 %reduce-scatter.22.cloned.1.call-start = ((), (), s32[]{:S(2)}) async-start(), calls=%async_computation.27 | async-start | bytes 5242880 | tf_op jit(solution)/shard_map/while/body/eval_jaxpr/reduce_scatter | solution.py:286
  2196.3 374.5 %reduce-scatter.24.cloned.1.call-start = ((), (), s32[]{:S(2)}) async-start(), calls=%async_computation.28 | async-start | bytes 5242880 | tf_op jit(solution)/shard_map/while/body/eval_jaxpr/reduce_scatter | solution.py:289
  2211.0 363.7 %reduce-scatter.26.cloned.1.call-start = ((), (), s32[]{:S(2)}) async-start(), calls=%async_computation.29 | async-start | bytes 1310720 | tf_op jit(solution)/shard_map/while/body/eval_jaxpr/reduce_scatter | solution.py:294
  2238.5 338.2 %reduce-scatter.18.cloned.1.call-start = ((), (), s32[]{:S(2)}) async-start(), calls=%async_computation.25 | async-start | bytes 1310720 | tf_op jit(solution)/shard_map/while/body/eval_jaxpr/reduce_scatter | solution.py:280
  2514.9 141.8 %reduce-scatter.30.cloned.1.call-start = ((), (), s32[]{:S(2)}) async-start(), calls=%async_computation.31 | async-start | bytes 9437184 | tf_op jit(solution)/shard_map/while/body/eval_jaxpr/reduce_scatter | solution.py:221
  2548.4 183.1 %reduce-scatter.32.cloned.1.call-start = ((), (), s32[]{:S(2)}) async-start(), calls=%async_computation.32 | async-start | bytes 9437184 | tf_op jit(solution)/shard_map/while/body/eval_jaxpr/reduce_scatter | solution.py:183
  (120 other events, 6411.1 us)
Sparse Core Ops, SparseCore 0:
  10.2 30.6 all-gather.27
  42.7 53.8 all-gather.23
  98.2 27.9 all-gather.25
  247.2 70.7 reduce-scatter.11
  319.6 80.7 all-gather.37
  402.5 52.9 all-gather.39
  457.1 80.7 all-gather.35
  539.8 52.9 all-gather.33
  594.4 80.7 all-gather.41
  727.9 69.8 reduce-scatter.13
  804.8 54.3 all-gather.43
  861.4 76.7 reduce-scatter.27
  940.4 77.2 reduce-scatter.21
  1019.9 77.2 reduce-scatter.23
  1223.6 69.9 reduce-scatter.29
  1297.0 71.2 reduce-scatter.31
  1376.3 27.9 all-gather.27
  1406.0 53.8 all-gather.23
  1461.5 27.9 all-gather.25
  1610.5 70.7 reduce-scatter.11
  1683.0 80.7 all-gather.37
  1765.6 52.9 all-gather.39
  1820.2 80.7 all-gather.35
  1903.1 52.9 all-gather.33
  1957.5 80.7 all-gather.41
  2091.1 69.8 reduce-scatter.13
  2168.0 54.3 all-gather.43
  2224.5 76.7 reduce-scatter.27
  2303.6 77.2 reduce-scatter.21
  2383.2 77.2 reduce-scatter.23
  2586.7 69.9 reduce-scatter.29
  2660.2 71.2 reduce-scatter.31
  (12 shorter events, 322.1 us)
where the time goes:
time: 2790 us
  waiting for transfers between devices  1440 us (52%)
  matrix products  787 us (28%)
  other arithmetic  254 us (9%)
  local copies, waits for them, and re-layouts  161 us (6%)
  blocking collectives  89.3 us (3%)
  loops' own time  37.8 us (1%)
    dot_general x14, matrix products, mat_back(): lax.dot_general(left_op, right_op, (((1,), (1,)), ((), ())), preferred_el...  169 us
    all_gather x2, waiting for transfers between devices, fetch_weights(): lax.all_gather(w_down, 'narrow', axis=1, tiled=True)  155 us
    dot_general x14, matrix products, mat_plain(): return jnp.dot(left_op, right_op, preferred_element_type=jnp.float32)  151 us
    reduce_scatter x2, waiting for transfers between devices, one_row(): lax.psum_scatter(rounded(mat_plain(hidden, w_down)).astype(jnp.bfloat16),...  145 us
    reduce_scatter x2, waiting for transfers between devices, one_row(): lax.psum_scatter(rounded(mat_back(query_raw, w_query) + mat_back(key_raw,...  144 us
    reduce_scatter x2, waiting for transfers between devices, one_row(): lax.psum_scatter(rounded(mat_back(grad_gate_pre, w_gate) + mat_back(grad_...  140 us
    all_gather x2, waiting for transfers between devices, fetch_weights(): lax.all_gather(w_up, 'narrow', axis=0, tiled=True)  136 us
    all_gather x2, waiting for transfers between devices, fetch_weights(): lax.all_gather(w_gate, 'narrow', axis=0, tiled=True)  135 us
  transfers between devices with their start and end apart: 44, of which 30 were waited for; matrix products, arithmetic and copies ran while one was open for 38% of the time, Pallas kernels for 0%

commit v1 on v0

--- a/solution.py
+++ b/solution.py
@@ -7,6 +7,17 @@
 EPS = 1e-05
 NEG = -1e30
 ROPE_BASE = 130000.0
+
+
+def pass_along(x, mesh_axis, dim):
+    size = lax.axis_size(mesh_axis)
+    route = [(i, (i + 1) % size) for i in range(size)]
+    shards = [x]
+    for stride in range(1, size):
+        shards = [lax.ppermute(shards[0], mesh_axis, route), *shards]
+    full = jnp.concatenate(shards, axis=dim)
+    shift = (lax.axis_index(mesh_axis) + 1) * shards[-1].shape[dim]
+    return jnp.roll(full, shift, axis=dim)
 
 
 def mat_plain(left_op, right_op):
@@ -186,7 +197,7 @@
         scatter_dimension=0,
         tiled=True,
     ).astype(jnp.float32)
-    grad_full = lax.all_gather(grad_row, "wide", axis=0, tiled=True)
+    grad_full = pass_along(grad_row, "wide", 0)
     grad_down = mat_outer(hidden, grad_full)
     grad_hidden = mat_back(grad_full, w_down)
     grad_gate_pre = (

time: 2790 us -> 2720 us (0.975)
  waiting for transfers between devices: 1440 us -> 1310 us
  local copies, waits for them, and re-layouts: 161 us -> 214 us
    ppermute x0 -> x14, waiting for transfers between devices: none -> 272 us  [pass_along(): shards = [lax.ppermute(shards[0], mesh_axis, route), *shards]]
    all_gather x2, waiting for transfers between devices: 135 us -> 0.01 us  [fetch_weights(): lax.all_gather(w_gate, 'narrow', axis=0, tiled=True)]
    all_gather x2, waiting for transfers between devices: 110 us -> 0.01 us  [one_row(): lax.all_gather((normed_mid * mlp_scale).astype(jnp.bfloat16), 'wide', axi...]
    all_gather x2 -> x0, waiting for transfers between devices: 110 us -> none  [one_row(): grad_full = lax.all_gather(grad_row, 'wide', axis=0, tiled=True)]
    while x226 -> x292, local copies, waits for them, and re-layouts: 20 us -> 70.5 us
    all_gather x2, waiting for transfers between devices: 136 us -> 103 us  [fetch_weights(): lax.all_gather(w_up, 'narrow', axis=0, tiled=True)]
  transfers between devices with their start and end apart: 44 -> 56, of which waited for: 30 -> 38; matrix products, arithmetic and copies ran while one was open for 38% -> 40% of each run, Pallas kernels for 0% -> 0%
where the time goes in v1:
time: 2720 us; the launch traced here: 2710 us
  waiting for transfers between devices  1310 us (48%)
  matrix products  793 us (29%)
  other arithmetic  255 us (9%)
  local copies, waits for them, and re-layouts  214 us (8%)
  blocking collectives  89.3 us (3%)
  loops' own time  37.8 us (1%)
    ppermute x14, waiting for transfers between devices, pass_along(): shards = [lax.ppermute(shards[0], mesh_axis, route), *shards]  272 us
    dot_general x14, matrix products, mat_back(): lax.dot_general(left_op, right_op, (((1,), (1,)), ((), ())), preferred_el...  189 us
    reduce_scatter x2, waiting for transfers between devices, one_row(): lax.psum_scatter(rounded(mat_plain(hidden, w_down)).astype(jnp.bfloat16),...  145 us
    reduce_scatter x2, waiting for transfers between devices, one_row(): lax.psum_scatter(rounded(mat_back(query_raw, w_query) + mat_back(key_raw,...  144 us
    reduce_scatter x2, waiting for transfers between devices, one_row(): lax.psum_scatter(rounded(mat_back(grad_gate_pre, w_gate) + mat_back(grad_...  140 us
    dot_general x14, matrix products, mat_plain(): return jnp.dot(left_op, right_op, preferred_element_type=jnp.float32)  136 us
    dot_general x14, matrix products, mat_outer(): lax.dot_general(left_op, right_op, (((0,), (0,)), ((), ())), preferred_el...  135 us
    all_gather x2, waiting for transfers between devices, fetch_weights(): lax.all_gather(w_down, 'narrow', axis=1, tiled=True)  133 us
  transfers between devices with their start and end apart: 56, of which 38 were waited for; matrix products, arithmetic and copies ran while one was open for 40% of the time, Pallas kernels for 0%

profile of v1, /device:TPU:0, one launch (start us, length us, event | category | flops | bytes accessed | tf_op | source)
XLA Modules:
  0.0 2711.5 jit_solution(15680011454860442477)
XLA Ops:
  7.3 2656.5 %while.91 = (s32[]{:T(128)}, f32[512,256]{1,0:T(8,128)}, f32[512,256]{1,0:T(8,128)}, f32[512,256]{1,0:T(8,128)}, f32[512,1024]{1,0:T(8,128)}, /*index=5*/f32[512...) while((s32[]{:T(128)}, f32[512,256]{1,0:T(8,128)}, ...), condition=%wide.region_27.28_spmd.clone, body=%wide.region_0.27_spmd.clone.sunk | while | flops 107088232448 | bytes 1288338432 | solution.py:336
  40.8 55.8 %all-gather.19.cloned.1.call-done = bf16[2048,2048]{1,0:T(8,128)(2,1)} async-done(((bf16[256,2048]{1,0:T(8,128)(2,1)}), bf16[2048,2048]{1,0:T(8,128)(2,1)}) %all-gather.19.cloned.1.call-update) | async-done | bytes 8388624 | tf_op jit(solution)/shard_map/while/body/eval_jaxpr/all_gather | solution.py:168
  102.6 23.6 all-gather.21.cloned.1.call-done
  133.0 22.1 all-gather.25.cloned.1.call-done
  161.1 74.7 %while.92 = (s32[]{:T(128)}, bf16[4,512,4,64]{1,3,2,0:T(8,128)(2,1)}, f32[4,4,512]{2,1,0:T(4,128)}, s32[4]{0:T(128)S(1)}, s32[2048]{0:T(1024)}, /*index=5*/bf16[...) while((s32[]{:T(128)}, ...), condition=%wide.region_7.7_spmd, body=%wide.region_4.6_spmd.sunk | while | flops 1127217664 | bytes 65874156 | solution.py:102
  260.1 58.0 %reduce-scatter.12.cloned.1.call-done = bf16[256,2048]{1,0:T(8,128)(2,1)} async-done(((bf16[2048,2048]{1,0:T(8,128)(2,1)}), bf16[256,2048]{1,0:T(8,128)(2,1)}) %reduce-scatter.12.cloned.1.call-update) | async-done | bytes 1048592 | tf_op jit(solution)/shard_map/while/body/eval_jaxpr/reduce_scatter | solution.py:178
  404.6 26.5 collective-permute-done.5
  431.2 33.7 %collective-permute-done.6 = bf16[256,2048]{1,0:T(8,128)(2,1)} collective-permute-done((bf16[256,2048]{1,0:T(8,128)(2,1)}, bf16[256,2048]{1,0:T(8,128)(2,1)}, u32[]{:S(2)}, u32[]{:S(2)}) %collective-permute-start.6) | collective-permute-done | bytes 1048608 | tf_op jit(solution)/shard_map/while/body/eval_jaxpr/ppermute | solution.py:17
  501.7 51.6 %all-gather.31.cloned.1.call-done = bf16[2048,1024]{1,0:T(8,128)(2,1)} async-done(((bf16[512,1024]{1,0:T(8,128)(2,1)}), bf16[2048,1024]{1,0:T(8,128)(2,1)}) %all-gather.31.cloned.1.call-update) | async-done | bytes 4194320 | tf_op jit(solution)/shard_map/while/body/eval_jaxpr/all_gather | solution.py:276
  567.7 66.4 %all-gather.35.cloned.1.call-done = bf16[1024,2048]{1,0:T(8,128)(2,1)} async-done(((bf16[1024,512]{1,0:T(8,128)(2,1)}), bf16[1024,2048]{1,0:T(8,128)(2,1)}) %all-gather.35.cloned.1.call-update) | async-done | bytes 4194320 | tf_op jit(solution)/shard_map/while/body/eval_jaxpr/all_gather | solution.py:282
  634.1 24.1 multiply_convert_fusion.9
  673.6 16.0 add_convert_fusion.9
  689.8 70.0 %reduce-scatter.14.cloned.1.call-done = bf16[256,2048]{1,0:T(8,128)(2,1)} async-done(((bf16[2048,2048]{1,0:T(8,128)(2,1)}), bf16[256,2048]{1,0:T(8,128)(2,1)}) %reduce-scatter.14.cloned.1.call-update) | async-done | bytes 1048592 | tf_op jit(solution)/shard_map/while/body/eval_jaxpr/reduce_scatter | solution.py:209
  837.3 249.8 %while.93 = (s32[]{:T(128)}, f32[2048,4,64]{0,2,1:T(8,128)}, f32[2048,4,64]{0,2,1:T(8,128)}, f32[4,512,4,64]{1,0,3,2:T(4,128)}, bf16[4,512,4,64]{1,3,2,0:T(8,128...) while((s32[]{:T(128)}, f32[2048,4,64]{0,2,1:T(8,128)}, ...), condition=%wide.region_14.14_spmd.clone, body=%wide.region_12.13_spmd.clone.sunk | while | flops 2753165824 | bytes 183044368 | solution.py:145
  1184.1 71.9 %reduce-scatter.30.cloned.1.call-done = bf16[256,2048]{1,0:T(8,128)(2,1)} async-done(((bf16[2048,2048]{1,0:T(8,128)(2,1)}), bf16[256,2048]{1,0:T(8,128)(2,1)}) %reduce-scatter.30.cloned.1.call-update) | async-done | bytes 1048592 | tf_op jit(solution)/shard_map/while/body/eval_jaxpr/reduce_scatter | solution.py:232
  1258.0 72.7 %reduce-scatter.32.cloned.1.call-done = bf16[256,2048]{1,0:T(8,128)(2,1)} async-done(((bf16[2048,2048]{1,0:T(8,128)(2,1)}), bf16[256,2048]{1,0:T(8,128)(2,1)}) %reduce-scatter.32.cloned.1.call-update) | async-done | bytes 1048592 | tf_op jit(solution)/shard_map/while/body/eval_jaxpr/reduce_scatter | solution.py:194
  1366.6 55.8 %all-gather.19.cloned.1.call-done = bf16[2048,2048]{1,0:T(8,128)(2,1)} async-done(((bf16[256,2048]{1,0:T(8,128)(2,1)}), bf16[2048,2048]{1,0:T(8,128)(2,1)}) %all-gather.19.cloned.1.call-update) | async-done | bytes 8388624 | tf_op jit(solution)/shard_map/while/body/eval_jaxpr/all_gather | solution.py:168
  1428.4 23.4 all-gather.21.cloned.1.call-done
  1458.6 22.2 all-gather.25.cloned.1.call-done
  1486.8 75.0 %while.92 = (s32[]{:T(128)}, bf16[4,512,4,64]{1,3,2,0:T(8,128)(2,1)}, f32[4,4,512]{2,1,0:T(4,128)}, s32[4]{0:T(128)S(1)}, s32[2048]{0:T(1024)}, /*index=5*/bf16[...) while((s32[]{:T(128)}, ...), condition=%wide.region_7.7_spmd, body=%wide.region_4.6_spmd.sunk | while | flops 1127217664 | bytes 65874156 | solution.py:102
  1586.1 58.0 %reduce-scatter.12.cloned.1.call-done = bf16[256,2048]{1,0:T(8,128)(2,1)} async-done(((bf16[2048,2048]{1,0:T(8,128)(2,1)}), bf16[256,2048]{1,0:T(8,128)(2,1)}) %reduce-scatter.12.cloned.1.call-update) | async-done | bytes 1048592 | tf_op jit(solution)/shard_map/while/body/eval_jaxpr/reduce_scatter | solution.py:178
  1730.6 26.5 collective-permute-done.5
  1757.2 33.7 %collective-permute-done.6 = bf16[256,2048]{1,0:T(8,128)(2,1)} collective-permute-done((bf16[256,2048]{1,0:T(8,128)(2,1)}, bf16[256,2048]{1,0:T(8,128)(2,1)}, u32[]{:S(2)}, u32[]{:S(2)}) %collective-permute-start.6) | collective-permute-done | bytes 1048608 | tf_op jit(solution)/shard_map/while/body/eval_jaxpr/ppermute | solution.py:17
  1827.7 51.4 %all-gather.31.cloned.1.call-done = bf16[2048,1024]{1,0:T(8,128)(2,1)} async-done(((bf16[512,1024]{1,0:T(8,128)(2,1)}), bf16[2048,1024]{1,0:T(8,128)(2,1)}) %all-gather.31.cloned.1.call-update) | async-done | bytes 4194320 | tf_op jit(solution)/shard_map/while/body/eval_jaxpr/all_gather | solution.py:276
  1893.6 66.5 %all-gather.35.cloned.1.call-done = bf16[1024,2048]{1,0:T(8,128)(2,1)} async-done(((bf16[1024,512]{1,0:T(8,128)(2,1)}), bf16[1024,2048]{1,0:T(8,128)(2,1)}) %all-gather.35.cloned.1.call-update) | async-done | bytes 4194320 | tf_op jit(solution)/shard_map/while/body/eval_jaxpr/all_gather | solution.py:282
  1960.1 23.9 multiply_convert_fusion.9
  1999.4 16.3 add_convert_fusion.9
  2015.8 70.0 %reduce-scatter.14.cloned.1.call-done = bf16[256,2048]{1,0:T(8,128)(2,1)} async-done(((bf16[2048,2048]{1,0:T(8,128)(2,1)}), bf16[256,2048]{1,0:T(8,128)(2,1)}) %reduce-scatter.14.cloned.1.call-update) | async-done | bytes 1048592 | tf_op jit(solution)/shard_map/while/body/eval_jaxpr/reduce_scatter | solution.py:209
  2163.4 249.8 %while.93 = (s32[]{:T(128)}, f32[2048,4,64]{0,2,1:T(8,128)}, f32[2048,4,64]{0,2,1:T(8,128)}, f32[4,512,4,64]{1,0,3,2:T(4,128)}, bf16[4,512,4,64]{1,3,2,0:T(8,128...) while((s32[]{:T(128)}, f32[2048,4,64]{0,2,1:T(8,128)}, ...), condition=%wide.region_14.14_spmd.clone, body=%wide.region_12.13_spmd.clone.sunk | while | flops 2753165824 | bytes 183044368 | solution.py:145
  2510.3 71.9 %reduce-scatter.30.cloned.1.call-done = bf16[256,2048]{1,0:T(8,128)(2,1)} async-done(((bf16[2048,2048]{1,0:T(8,128)(2,1)}), bf16[256,2048]{1,0:T(8,128)(2,1)}) %reduce-scatter.30.cloned.1.call-update) | async-done | bytes 1048592 | tf_op jit(solution)/shard_map/while/body/eval_jaxpr/reduce_scatter | solution.py:232
  2584.2 72.7 %reduce-scatter.32.cloned.1.call-done = bf16[256,2048]{1,0:T(8,128)(2,1)} async-done(((bf16[2048,2048]{1,0:T(8,128)(2,1)}), bf16[256,2048]{1,0:T(8,128)(2,1)}) %reduce-scatter.32.cloned.1.call-update) | async-done | bytes 1048592 | tf_op jit(solution)/shard_map/while/body/eval_jaxpr/reduce_scatter | solution.py:194
  2663.8 39.7 %all-reduce.2 = (f32[2048]{0:T(1024)S(1)}, f32[2048]{0:T(1024)S(1)}) all-reduce(f32[2048]{0:T(1024)} %get-tuple-element.420, f32[2048]{0:T(1024)} %get-tuple-element.425), channel_id=13, replica_groups=mesh['narrow'=4,'wide'=8] {'narrow','wide'}, use_global_device_ids=true, to_apply=%region_28.29.clone | all-reduce | flops 4096 | bytes 32768
  (739 shorter events, 1435.3 us)
Async XLA Ops:
  28.2 126.9 %all-gather.25.cloned.1.call-start = ((), (), s32[]{:S(2)}) async-start(), calls=%async_computation.14 | async-start | bytes 1310720 | tf_op jit(solution)/shard_map/while/body/eval_jaxpr/all_gather | solution.py:274
  28.8 211.1 %all-gather.27.cloned.1.call-start = ((), (), s32[]{:S(2)}) async-start(), calls=%async_computation.15 | async-start | bytes 1310720 | tf_op jit(solution)/shard_map/while/body/eval_jaxpr/all_gather | solution.py:281
  29.4 288.7 %reduce-scatter.12.cloned.1.call-start = ((), (), s32[]{:S(2)}) async-start(), calls=%async_computation.16 | async-start | bytes 9437184 | tf_op jit(solution)/shard_map/while/body/eval_jaxpr/reduce_scatter | solution.py:178
  247.2 240.0 %all-gather.33.cloned.1.call-start = ((), (), s32[]{:S(2)}) async-start(), calls=%async_computation.19 | async-start | bytes 5242880 | tf_op jit(solution)/shard_map/while/body/eval_jaxpr/all_gather | solution.py:275
  248.0 239.3 %all-gather.29.cloned.1.call-start = ((), (), s32[]{:S(2)}) async-start(), calls=%async_computation.17 | async-start | bytes 9437184 | tf_op jit(solution)/shard_map/while/body/eval_jaxpr/all_gather | solution.py:186
  322.4 230.9 %all-gather.31.cloned.1.call-start = ((), (), s32[]{:S(2)}) async-start(), calls=%async_computation.18 | async-start | bytes 5242880 | tf_op jit(solution)/shard_map/while/body/eval_jaxpr/all_gather | solution.py:276
  324.9 309.3 %all-gather.35.cloned.1.call-start = ((), (), s32[]{:S(2)}) async-start(), calls=%async_computation.20 | async-start | bytes 5242880 | tf_op jit(solution)/shard_map/while/body/eval_jaxpr/all_gather | solution.py:282
  431.1 328.6 %reduce-scatter.14.cloned.1.call-start = ((), (), s32[]{:S(2)}) async-start(), calls=%async_computation.21 | async-start | bytes 9437184 | tf_op jit(solution)/shard_map/while/body/eval_jaxpr/reduce_scatter | solution.py:209
  689.7 131.5 %all-gather.37.cloned.1.call-start = ((), (), s32[]{:S(2)}) async-start(), calls=%async_computation.22 | async-start | bytes 9437184 | tf_op jit(solution)/shard_map/while/body/eval_jaxpr/all_gather | solution.py:220
  766.6 395.6 %reduce-scatter.28.cloned.1.call-start = ((), (), s32[]{:S(2)}) async-start(), calls=%async_computation.29 | async-start | bytes 5242880 | tf_op jit(solution)/shard_map/while/body/eval_jaxpr/reduce_scatter | solution.py:308
  780.7 384.9 %reduce-scatter.22.cloned.1.call-start = ((), (), s32[]{:S(2)}) async-start(), calls=%async_computation.26 | async-start | bytes 5242880 | tf_op jit(solution)/shard_map/while/body/eval_jaxpr/reduce_scatter | solution.py:297
  795.3 374.2 %reduce-scatter.24.cloned.1.call-start = ((), (), s32[]{:S(2)}) async-start(), calls=%async_computation.27 | async-start | bytes 5242880 | tf_op jit(solution)/shard_map/while/body/eval_jaxpr/reduce_scatter | solution.py:300
  809.9 362.9 %reduce-scatter.26.cloned.1.call-start = ((), (), s32[]{:S(2)}) async-start(), calls=%async_computation.28 | async-start | bytes 1310720 | tf_op jit(solution)/shard_map/while/body/eval_jaxpr/reduce_scatter | solution.py:305
  837.3 337.4 %reduce-scatter.18.cloned.1.call-start = ((), (), s32[]{:S(2)}) async-start(), calls=%async_computation.24 | async-start | bytes 1310720 | tf_op jit(solution)/shard_map/while/body/eval_jaxpr/reduce_scatter | solution.py:291
  1114.5 141.5 %reduce-scatter.30.cloned.1.call-start = ((), (), s32[]{:S(2)}) async-start(), calls=%async_computation.30 | async-start | bytes 9437184 | tf_op jit(solution)/shard_map/while/body/eval_jaxpr/reduce_scatter | solution.py:232
  1147.9 182.8 %reduce-scatter.32.cloned.1.call-start = ((), (), s32[]{:S(2)}) async-start(), calls=%async_computation.31 | async-start | bytes 9437184 | tf_op jit(solution)/shard_map/while/body/eval_jaxpr/reduce_scatter | solution.py:194
  1354.9 125.9 %all-gather.25.cloned.1.call-start = ((), (), s32[]{:S(2)}) async-start(), calls=%async_computation.14 | async-start | bytes 1310720 | tf_op jit(solution)/shard_map/while/body/eval_jaxpr/all_gather | solution.py:274
  1355.6 210.2 %all-gather.27.cloned.1.call-start = ((), (), s32[]{:S(2)}) async-start(), calls=%async_computation.15 | async-start | bytes 1310720 | tf_op jit(solution)/shard_map/while/body/eval_jaxpr/all_gather | solution.py:281
  1356.2 287.9 %reduce-scatter.12.cloned.1.call-start = ((), (), s32[]{:S(2)}) async-start(), calls=%async_computation.16 | async-start | bytes 9437184 | tf_op jit(solution)/shard_map/while/body/eval_jaxpr/reduce_scatter | solution.py:178
  1573.2 240.1 %all-gather.33.cloned.1.call-start = ((), (), s32[]{:S(2)}) async-start(), calls=%async_computation.19 | async-start | bytes 5242880 | tf_op jit(solution)/shard_map/while/body/eval_jaxpr/all_gather | solution.py:275
  1573.9 239.3 %all-gather.29.cloned.1.call-start = ((), (), s32[]{:S(2)}) async-start(), calls=%async_computation.17 | async-start | bytes 9437184 | tf_op jit(solution)/shard_map/while/body/eval_jaxpr/all_gather | solution.py:186
  1648.4 230.7 %all-gather.31.cloned.1.call-start = ((), (), s32[]{:S(2)}) async-start(), calls=%async_computation.18 | async-start | bytes 5242880 | tf_op jit(solution)/shard_map/while/body/eval_jaxpr/all_gather | solution.py:276
  1650.8 309.2 %all-gather.35.cloned.1.call-start = ((), (), s32[]{:S(2)}) async-start(), calls=%async_computation.20 | async-start | bytes 5242880 | tf_op jit(solution)/shard_map/while/body/eval_jaxpr/all_gather | solution.py:282
  1757.1 328.6 %reduce-scatter.14.cloned.1.call-start = ((), (), s32[]{:S(2)}) async-start(), calls=%async_computation.21 | async-start | bytes 9437184 | tf_op jit(solution)/shard_map/while/body/eval_jaxpr/reduce_scatter | solution.py:209
  2015.7 131.5 %all-gather.37.cloned.1.call-start = ((), (), s32[]{:S(2)}) async-start(), calls=%async_computation.22 | async-start | bytes 9437184 | tf_op jit(solution)/shard_map/while/body/eval_jaxpr/all_gather | solution.py:220
  2092.6 395.6 %reduce-scatter.28.cloned.1.call-start = ((), (), s32[]{:S(2)}) async-start(), calls=%async_computation.29 | async-start | bytes 5242880 | tf_op jit(solution)/shard_map/while/body/eval_jaxpr/reduce_scatter | solution.py:308
  2106.7 385.0 %reduce-scatter.22.cloned.1.call-start = ((), (), s32[]{:S(2)}) async-start(), calls=%async_computation.26 | async-start | bytes 5242880 | tf_op jit(solution)/shard_map/while/body/eval_jaxpr/reduce_scatter | solution.py:297
  2121.0 375.1 %reduce-scatter.24.cloned.1.call-start = ((), (), s32[]{:S(2)}) async-start(), calls=%async_computation.27 | async-start | bytes 5242880 | tf_op jit(solution)/shard_map/while/body/eval_jaxpr/reduce_scatter | solution.py:300
  2135.7 364.3 %reduce-scatter.26.cloned.1.call-start = ((), (), s32[]{:S(2)}) async-start(), calls=%async_computation.28 | async-start | bytes 1310720 | tf_op jit(solution)/shard_map/while/body/eval_jaxpr/reduce_scatter | solution.py:305
  2163.3 338.9 %reduce-scatter.18.cloned.1.call-start = ((), (), s32[]{:S(2)}) async-start(), calls=%async_computation.24 | async-start | bytes 1310720 | tf_op jit(solution)/shard_map/while/body/eval_jaxpr/reduce_scatter | solution.py:291
  2440.5 141.7 %reduce-scatter.30.cloned.1.call-start = ((), (), s32[]{:S(2)}) async-start(), calls=%async_computation.30 | async-start | bytes 9437184 | tf_op jit(solution)/shard_map/while/body/eval_jaxpr/reduce_scatter | solution.py:232
  2473.9 183.0 %reduce-scatter.32.cloned.1.call-start = ((), (), s32[]{:S(2)}) async-start(), calls=%async_computation.31 | async-start | bytes 9437184 | tf_op jit(solution)/shard_map/while/body/eval_jaxpr/reduce_scatter | solution.py:194
  (150 other events, 6530.8 us)
Sparse Core Ops, SparseCore 0:
  10.2 30.6 all-gather.22
  42.7 53.8 all-gather.18
  98.2 27.9 all-gather.20
  247.3 70.7 reduce-scatter.11
  319.8 80.7 all-gather.32
  402.6 68.2 all-gather.28
  472.6 80.6 all-gather.30
  554.8 79.2 all-gather.34
  689.8 69.8 reduce-scatter.13
  766.8 54.3 all-gather.36
  823.5 76.8 reduce-scatter.27
  902.6 77.1 reduce-scatter.21
  981.9 77.2 reduce-scatter.23
  1061.5 27.6 reduce-scatter.25
  1186.0 69.9 reduce-scatter.29
  1259.4 71.2 reduce-scatter.31
  1338.6 27.8 all-gather.22
  1368.5 53.8 all-gather.18
  1423.8 27.9 all-gather.20
  1573.3 70.7 reduce-scatter.11
  1645.7 80.7 all-gather.32
  1728.6 68.2 all-gather.28
  1798.4 80.6 all-gather.30
  1880.7 79.2 all-gather.34
  2015.8 69.8 reduce-scatter.13
  2092.8 54.3 all-gather.36
  2149.5 76.7 reduce-scatter.27
  2228.7 77.2 reduce-scatter.21
  2308.1 77.2 reduce-scatter.23
  2387.6 27.6 reduce-scatter.25
  2512.2 69.9 reduce-scatter.29
  2585.6 71.2 reduce-scatter.31
  (10 shorter events, 266.8 us)
